TPU v7x, 32 devices: a whole 2x2x4 slice. The times are simulated.
32 devices in a mesh: dp: 8 (over z, x), seq: 4 (over y, core).
Axes of the slice: x: 2, y: 2, z: 4, core: 2. Of those that a mesh axis runs over, the one named last changes fastest.
Arguments:
- short_input: bfloat16 [192, 128, 1024], P(('dp', 'seq')), may hold values from -6 to 6
- long_input: bfloat16 [16, 512, 1024], P('dp', 'seq'), may hold values from -6 to 6
- short_cotangent: bfloat16 [192, 128, 1024], P(('dp', 'seq')), may hold values from -6 to 6
- long_cotangent: bfloat16 [16, 512, 1024], P('dp', 'seq'), may hold values from -6 to 6
- short_lengths: int32 [192], P(('dp', 'seq')), may hold values from 32 to 128, as said below
- long_lengths: int32 [16], P('dp'), may hold values from 128 to 512, as said below
- query_weight: float32 [1024, 1024], P(('dp', 'seq')), may hold values from -0.1875 to 0.1875
- key_weight: float32 [1024, 1024], P(('dp', 'seq')), may hold values from -0.1875 to 0.1875
- value_weight: float32 [1024, 1024], P(('dp', 'seq')), may hold values from -0.1875 to 0.1875
- output_weight: float32 [1024, 1024], P(('dp', 'seq')), may hold values from -0.75 to 0.75
- upward_weight: float32 [1024, 4096], P(('dp', 'seq')), may hold values from -0.1875 to 0.1875
- downward_weight: float32 [4096, 1024], P(('dp', 'seq')), may hold values from -0.09375 to 0.09375
- query_bias: float32 [1024], replicated, may hold values from -3 to 3
- value_bias: float32 [1024], replicated, may hold values from -3 to 3
- output_bias: float32 [1024], replicated, may hold values from -3 to 3
- upward_bias: float32 [4096], replicated, may hold values from -3 to 3
- downward_bias: float32 [1024], replicated, may hold values from -3 to 3
- first_gain: float32 [1024], replicated, may hold values from 0.25 to 1.75
- first_shift: float32 [1024], replicated, may hold values from -3 to 3
- second_gain: float32 [1024], replicated, may hold values from 0.25 to 1.75
- second_shift: float32 [1024], replicated, may hold values from -3 to 3
Outputs:
- short_output: bfloat16 [192, 128, 1024], P(('dp', 'seq'))
- long_output: bfloat16 [16, 512, 1024], P('dp', 'seq')
- short_grad: bfloat16 [192, 128, 1024], P(('dp', 'seq'))
- long_grad: bfloat16 [16, 512, 1024], P('dp', 'seq')
- query_delta: float32 [1024], replicated
- value_delta: float32 [1024], replicated
- output_delta: float32 [1024], replicated
- upward_delta: float32 [4096], replicated
- downward_delta: float32 [1024], replicated
- first_delta: float32 [1024], replicated
- second_delta: float32 [1024], replicated
Inputs may be any that keep to these rules, and one draw needn't show every extreme that they name: `short_lengths`: some short sequence has all 128 positions. `long_lengths`: some long sequence has all 512 positions.
All inputs are finite; a program needn't handle non-finite values.
Results may differ from a plain program's by a relative error of at most 0.013.
The roundings to bfloat16 on the way count: a program that leaves them out, or rounds other values in their place, can miss the bound.
Values may be sent and summed in bfloat16 or wider, within the bound.
A program may use at most 192 MiB of HBM per device.

v0:
```python
import jax
import jax.numpy as jnp
from jax import lax
from jax.sharding import PartitionSpec as P

HEADS = 16
HEAD = 64
epsilon = 1e-12
masked = -1e30


def forward_product(left, right):
    return jnp.dot(left, right, preferred_element_type=jnp.float32)


def backward_product(left, right):
    return lax.dot_general(
        left, right, (((left.ndim - 1,), (1,)), ((), ())), preferred_element_type=jnp.float32
    )


def exact_backward(left, right):
    return lax.dot_general(
        left,
        right,
        (((left.ndim - 1,), (1,)), ((), ())),
        precision=lax.Precision.HIGHEST,
        preferred_element_type=jnp.float32,
    )


def norm_apply(value, gain, shift):
    center = value - jnp.mean(value, axis=-1, keepdims=True)
    spread = jnp.mean(center * center, axis=-1, keepdims=True)
    return center * lax.rsqrt(spread + epsilon) * gain + shift


def token_total(value):
    return jnp.sum(value, axis=(0, 1))


def keep_local(first_part, second_part):
    return (first_part, second_part)


def spread_long(key_rows, values):
    return (
        lax.all_gather(key_rows, "seq", axis=1, tiled=True),
        lax.all_gather(values, "seq", axis=1, tiled=True),
    )


def settle_each(value):
    return lax.psum(value, ("dp", "seq"))


def finish_local(key_terms, value_terms, key_exact, value_exact, settle):
    value_delta = settle(token_total(value_terms))
    through = exact_backward(key_terms, key_exact) + exact_backward(value_terms, value_exact)
    return (through, value_delta)


def finish_summed(key_terms, value_terms, key_exact, value_exact, settle):
    key_grad, value_grad = (
        lax.psum_scatter(
            key_terms.astype(jnp.bfloat16), "seq", scatter_dimension=1, tiled=True
        ).astype(jnp.float32),
        lax.psum_scatter(
            value_terms.astype(jnp.bfloat16), "seq", scatter_dimension=1, tiled=True
        ).astype(jnp.float32),
    )
    value_delta = settle(token_total(value_grad))
    through = exact_backward(key_grad, key_exact) + exact_backward(value_grad, value_exact)
    return (through, value_delta)


def recompute(inputs, usable, weights, params, spread):
    query_weight, key_weight, value_weight, output_weight, upward_weight, downward_weight = weights
    (
        query_bias,
        value_bias,
        output_bias,
        upward_bias,
        downward_bias,
        first_gain,
        first_shift,
        second_gain,
        second_shift,
    ) = params
    number, seqlen, breadth = inputs.shape
    queries = (forward_product(inputs, query_weight) + query_bias).astype(jnp.bfloat16)
    key_rows = forward_product(inputs, key_weight).astype(jnp.bfloat16)
    values = (forward_product(inputs, value_weight) + value_bias).astype(jnp.bfloat16)
    key_all, value_all = spread(key_rows, values)
    query_heads = queries.reshape(number, seqlen, HEADS, HEAD)
    key_heads = key_all.reshape(number, key_all.shape[1], HEADS, HEAD)
    value_heads = value_all.reshape(number, value_all.shape[1], HEADS, HEAD)
    scores = jnp.einsum(
        "nqhd,nkhd->nhqk", query_heads, key_heads, preferred_element_type=jnp.float32
    ) * HEAD ** (-0.5)
    scores = jnp.where(usable[:, None, None, :], scores, masked)
    attention = jax.nn.softmax(scores, axis=-1)
    attention_low = attention.astype(jnp.bfloat16)
    blended = jnp.einsum(
        "nhqk,nkhd->nqhd", attention_low, value_heads, preferred_element_type=jnp.float32
    )
    blended = blended.reshape(number, seqlen, breadth).astype(jnp.bfloat16)
    residual = inputs.astype(jnp.float32) + forward_product(blended, output_weight) + output_bias
    normed = norm_apply(residual, first_gain, first_shift)
    pre_up = forward_product(normed.astype(jnp.bfloat16), upward_weight) + upward_bias
    active = jax.nn.gelu(pre_up, approximate=True).astype(jnp.bfloat16)
    ffn_sum = normed + forward_product(active, downward_weight) + downward_bias
    output = norm_apply(ffn_sum, second_gain, second_shift)
    return (
        query_heads,
        key_heads,
        value_heads,
        attention,
        attention_low,
        residual,
        pre_up,
        ffn_sum,
        output,
    )


def backprop(inputs, cotangent, usable, weights, params, spread, finish, settle):
    (
        query_heads,
        key_heads,
        value_heads,
        attention,
        attention_low,
        residual,
        pre_up,
        ffn_sum,
        output,
    ) = recompute(inputs, usable, weights, params, spread)
    query_weight, key_weight, value_weight, output_weight, upward_weight, downward_weight = weights
    (
        query_bias,
        value_bias,
        output_bias,
        upward_bias,
        downward_bias,
        first_gain,
        first_shift,
        second_gain,
        second_shift,
    ) = params
    number, seqlen, breadth = inputs.shape
    upstream = cotangent.astype(jnp.float32)
    second_pull = jax.vjp(lambda value: norm_apply(value, second_gain, second_shift), ffn_sum)[1]
    ffn_grad = second_pull(upstream)[0]
    second_delta = settle(token_total(upstream))
    downward_delta = settle(token_total(ffn_grad))
    active_grad = backward_product(ffn_grad.astype(jnp.bfloat16), downward_weight)
    gelu_pull = jax.vjp(lambda value: jax.nn.gelu(value, approximate=True), pre_up)[1]
    pre_grad = gelu_pull(active_grad)[0]
    upward_delta = settle(token_total(pre_grad))
    normed_grad = ffn_grad + backward_product(pre_grad.astype(jnp.bfloat16), upward_weight)
    first_delta = settle(token_total(normed_grad))
    first_pull = jax.vjp(lambda value: norm_apply(value, first_gain, first_shift), residual)[1]
    residual_grad = first_pull(normed_grad)[0]
    output_delta = settle(token_total(residual_grad))
    blended_grad = backward_product(residual_grad.astype(jnp.bfloat16), output_weight).astype(
        jnp.bfloat16
    )
    blended_grad = blended_grad.reshape(number, seqlen, HEADS, HEAD)
    prob_grad = jnp.einsum(
        "nqhd,nkhd->nhqk", blended_grad, value_heads, preferred_element_type=jnp.float32
    )
    score_grad = attention * (prob_grad - jnp.sum(prob_grad * attention, axis=-1, keepdims=True))
    score_grad = score_grad.astype(jnp.bfloat16)
    query_grad = jnp.einsum(
        "nhqk,nkhd->nqhd", score_grad, key_heads, preferred_element_type=jnp.float32
    )
    query_grad = query_grad.reshape(number, seqlen, breadth) * HEAD ** (-0.5)
    key_terms = jnp.einsum(
        "nhqk,nqhd->nkhd", score_grad, query_heads, preferred_element_type=jnp.float32
    )
    key_terms = key_terms.reshape(number, key_heads.shape[1], breadth) * HEAD ** (-0.5)
    value_terms = jnp.einsum(
        "nhqk,nqhd->nkhd", attention_low, blended_grad, preferred_element_type=jnp.float32
    )
    value_terms = value_terms.reshape(number, value_heads.shape[1], breadth)
    key_exact = key_weight.astype(jnp.float32)
    value_exact = value_weight.astype(jnp.float32)
    through, value_delta = finish(key_terms, value_terms, key_exact, value_exact, settle)
    query_delta = settle(token_total(query_grad))
    input_grad = (
        residual_grad + backward_product(query_grad.astype(jnp.bfloat16), query_weight) + through
    )
    deltas = (
        query_delta,
        value_delta,
        output_delta,
        upward_delta,
        downward_delta,
        first_delta,
        second_delta,
    )
    return (input_grad.astype(jnp.bfloat16), deltas)


def on_device(
    short_input,
    long_input,
    short_cotangent,
    long_cotangent,
    short_lengths,
    long_lengths,
    query_weight,
    key_weight,
    value_weight,
    output_weight,
    upward_weight,
    downward_weight,
    query_bias,
    value_bias,
    output_bias,
    upward_bias,
    downward_bias,
    first_gain,
    first_shift,
    second_gain,
    second_shift,
):
    params = (
        query_bias,
        value_bias,
        output_bias,
        upward_bias,
        downward_bias,
        first_gain,
        first_shift,
        second_gain,
        second_shift,
    )
    short_usable = jnp.arange(short_input.shape[1])[None, :] < short_lengths[:, None]
    long_span = long_input.shape[1] * lax.axis_size("seq")
    long_usable = jnp.arange(long_span)[None, :] < long_lengths[:, None]
    query_low = query_weight.astype(jnp.bfloat16)
    key_low = key_weight.astype(jnp.bfloat16)
    value_low = value_weight.astype(jnp.bfloat16)
    output_low = output_weight.astype(jnp.bfloat16)
    upward_low = upward_weight.astype(jnp.bfloat16)
    downward_low = downward_weight.astype(jnp.bfloat16)
    gathered = (
        lax.all_gather(query_low, ("dp", "seq"), axis=0, tiled=True),
        lax.all_gather(key_low, ("dp", "seq"), axis=0, tiled=True),
        lax.all_gather(value_low, ("dp", "seq"), axis=0, tiled=True),
        lax.all_gather(output_low, ("dp", "seq"), axis=0, tiled=True),
        lax.all_gather(upward_low, ("dp", "seq"), axis=0, tiled=True),
        lax.all_gather(downward_low, ("dp", "seq"), axis=0, tiled=True),
    )
    short_output = recompute(short_input, short_usable, gathered, params, keep_local)[-1]
    long_output = recompute(long_input, long_usable, gathered, params, spread_long)[-1]
    regathered = (
        lax.all_gather(query_low, ("dp", "seq"), axis=0, tiled=True),
        lax.all_gather(key_low, ("dp", "seq"), axis=0, tiled=True),
        lax.all_gather(value_low, ("dp", "seq"), axis=0, tiled=True),
        lax.all_gather(output_low, ("dp", "seq"), axis=0, tiled=True),
        lax.all_gather(upward_low, ("dp", "seq"), axis=0, tiled=True),
        lax.all_gather(downward_low, ("dp", "seq"), axis=0, tiled=True),
    )
    short_grad, short_deltas = backprop(
        short_input,
        short_cotangent,
        short_usable,
        regathered,
        params,
        keep_local,
        finish_local,
        settle_each,
    )
    long_grad, long_deltas = backprop(
        long_input,
        long_cotangent,
        long_usable,
        regathered,
        params,
        spread_long,
        finish_summed,
        settle_each,
    )
    summed = tuple(
        (first_part + second_part for first_part, second_part in zip(short_deltas, long_deltas))
    )
    return (
        short_output.astype(jnp.bfloat16),
        long_output.astype(jnp.bfloat16),
        short_grad,
        long_grad,
        summed[0],
        summed[1],
        summed[2],
        summed[3],
        summed[4],
        summed[5],
        summed[6],
    )


def solution(mesh):
    placed = (
        P(("dp", "seq"), None, None),
        P("dp", "seq", None),
        P(("dp", "seq"), None, None),
        P("dp", "seq", None),
        P(("dp", "seq")),
        P("dp"),
        P(("dp", "seq"), None),
        P(("dp", "seq"), None),
        P(("dp", "seq"), None),
        P(("dp", "seq"), None),
        P(("dp", "seq"), None),
        P(("dp", "seq"), None),
        P(),
        P(),
        P(),
        P(),
        P(),
        P(),
        P(),
        P(),
        P(),
    )
    return jax.shard_map(
        on_device,
        mesh=mesh,
        in_specs=placed,
        out_specs=(
            P(("dp", "seq"), None, None),
            P("dp", "seq", None),
            P(("dp", "seq"), None, None),
            P("dp", "seq", None),
            P(),
            P(),
            P(),
            P(),
            P(),
            P(),
            P(),
        ),
        check_vma=False,
    )
```

profile of v0, /device:TPU:0, one launch (start us, length us, event | category | flops | bytes accessed | tf_op | source)
XLA Modules:
  0.0 694.6 jit_solution(11124600776407439953)
XLA Ops:
  13.7 56.7 %all-gather.9.cloned.1.call-done = bf16[1024,1024]{1,0:T(8,128)(2,1)} async-done(((bf16[32,1024]{1,0:T(8,128)(2,1)}), bf16[1024,1024]{1,0:T(8,128)(2,1)}) %all-gather.9.cloned.1.call-update) | async-done | bytes 2097168 | tf_op jit(solution)/shard_map/all_gather | solution.py:252
  73.7 55.3 %all-gather.13.cloned.1.call-done = bf16[1024,1024]{1,0:T(8,128)(2,1)} async-done(((bf16[32,1024]{1,0:T(8,128)(2,1)}), bf16[1024,1024]{1,0:T(8,128)(2,1)}) %all-gather.13.cloned.1.call-update) | async-done | bytes 2097168 | tf_op jit(solution)/shard_map/all_gather | solution.py:251
  134.0 53.6 %all-gather.11.cloned.1.call-done = bf16[1024,1024]{1,0:T(8,128)(2,1)} async-done(((bf16[32,1024]{1,0:T(8,128)(2,1)}), bf16[1024,1024]{1,0:T(8,128)(2,1)}) %all-gather.11.cloned.1.call-update) | async-done | bytes 2097168 | tf_op jit(solution)/shard_map/all_gather | solution.py:250
  219.2 26.2 %all-gather.15.cloned.1.call-done = bf16[1024,1024]{1,0:T(8,128)(2,1)} async-done(((bf16[32,1024]{1,0:T(8,128)(2,1)}), bf16[1024,1024]{1,0:T(8,128)(2,1)}) %all-gather.15.cloned.1.call-update) | async-done | bytes 2097168 | tf_op jit(solution)/shard_map/all_gather | solution.py:253
  251.0 17.8 %all-gather.21.cloned.1.call-done = bf16[2,512,1024]{2,1,0:T(8,128)(2,1)} async-done(((bf16[2,128,1024]{2,1,0:T(8,128)(2,1)}), bf16[2,512,1024]{2,1,0:T(8,128)(2,1)}) %all-gather.21.cloned.1.call-update) | async-done | bytes 2097168 | tf_op jit(solution)/shard_map/all_gather | solution.py:49
  272.8 20.0 %all-gather.23.cloned.1.call-done = bf16[2,512,1024]{2,1,0:T(8,128)(2,1)} async-done(((bf16[2,128,1024]{2,1,0:T(8,128)(2,1)}), bf16[2,512,1024]{2,1,0:T(8,128)(2,1)}) %all-gather.23.cloned.1.call-update) | async-done | bytes 2097168 | tf_op jit(solution)/shard_map/all_gather | solution.py:48
  297.1 7.9 %fusion.219 = (f32[2,16,128]{2,1,0:T(8,128)S(1)}, f32[2,16,128,512]{3,2,1,0:T(8,128)}) fusion(pred[2,512]{1,0:T(4,128)(4,1)S(1)} %iota_compare_fusion, bf16[2,128,16,64]{1,3,2,0:T(8,128)(2,1)} %bitcast.210, bf16[2,512,16,64]{1,3,2,0:T(8,128)(2,1)} %bitcast.198), kind=kOutput, calls=%fused_computation.229 | convolution fusion | flops 276824576 | bytes 11027456 | tf_op jit(solution)/shard_map/sub | solution.py:102
  312.9 59.9 %all-gather.17.cloned.1.call-done = bf16[1024,4096]{1,0:T(8,128)(2,1)} async-done(((bf16[32,4096]{1,0:T(8,128)(2,1)}), bf16[1024,4096]{1,0:T(8,128)(2,1)}) %all-gather.17.cloned.1.call-update) | async-done | bytes 8388624 | tf_op jit(solution)/shard_map/all_gather | solution.py:254
  372.8 8.1 %fusion.30 = f32[2,128,4096]{2,1,0:T(8,128)} fusion(bf16[1024,4096]{1,0:T(8,128)(2,1)} %all-gather.17.cloned.1.call-done, f32[4096]{0:T(1024)S(1)} %copy-done.49, f32[2,128,1024]{2,1,0:T(8,128)} %copy-done.11, f32[1024]{0:T(1024)S(1)} %copy-done.53, f32[1024]{0:T(1024)S(1)} %copy-done.46, f32[2,128]{1,0:T(2,128)S(1)} %fusion.195, ...), kind=kOutput, calls=%fused_computation.43 | convolution fusion | flops 2149842944 | bytes 13658112 | tf_op jit(solution)/shard_map/dot_general | solution.py:13
  380.9 70.5 %all-gather.19.cloned.1.call-done = bf16[4096,1024]{1,0:T(8,128)(2,1)} async-done(((bf16[128,1024]{1,0:T(8,128)(2,1)}), bf16[4096,1024]{1,0:T(8,128)(2,1)}) %all-gather.19.cloned.1.call-update) | async-done | bytes 8388624 | tf_op jit(solution)/shard_map/all_gather | solution.py:255
  451.4 7.8 %fusion.221 = (f32[2,128]{1,0:T(2,128)S(1)}, f32[2,128,1024]{2,1,0:T(8,128)S(1)}) fusion(f32[1024]{0:T(1024)S(1)} %copy-done.52, bf16[4096,1024]{1,0:T(8,128)(2,1)} %all-gather.19.cloned.1.call-done, f32[2,128,4096]{2,1,0:T(8,128)} %fusion.30, f32[1024]{0:T(1024)S(1)} %copy-done.53, f32[1024]{0:T(1024)S(1)} %copy-done.46, f32[2,128]{1,0:T(2,128)S(1)} %fusion.195, ...), kind=kOutput, calls=%fused_computation.231 | convolution fusion | flops 2158755584 | bytes 14695424 | tf_op jit(solution)/shard_map/dot_general | solution.py:13
  460.1 8.3 %fusion.223 = (f32[4096]{0:T(1024)S(1)}, bf16[2,128,4096]{2,1,0:T(8,128)(2,1)S(1)}) fusion(f32[2,128,4096]{2,1,0:T(8,128)S(1)} %copy-done.56, bf16[4096,1024]{1,0:T(8,128)(2,1)} %all-gather.19.cloned.1.call-done, f32[2,128]{1,0:T(2,128)S(1)} %negate_multiply_fusion.3, f32[2,128]{1,0:T(2,128)S(1)} %get-tuple-element.42, ...), kind=kOutput, calls=%fused_computation.233 | convolution fusion | flops 2171858944 | bytes 16277504 | tf_op jit(solution)/shard_map/dot_general | solution.py:17
  476.9 5.9 fusion.95
  482.8 6.5 multiply_reduce_fusion
  493.3 13.0 %fusion.22 = f32[6,128,4096]{2,1,0:T(8,128)} fusion(bf16[1024,4096]{1,0:T(8,128)(2,1)} %all-gather.17.cloned.1.call-done, f32[6,128,1024]{2,1,0:T(8,128)S(1)} %get-tuple-element.47, f32[1024]{0:T(1024)S(1)} %copy-done.53, f32[1024]{0:T(1024)S(1)} %copy-done.46, f32[6,128]{1,0:T(8,128)S(1)} %fusion.193, f32[6,128]{1,0:T(8,128)S(1)} %broadcast_multiply_fusion.1), kind=kOutput, calls=%fused_computation.25 | convolution fusion | flops 6446383104 | bytes 24131584 | tf_op jit(solution)/shard_map/dot_general | solution.py:13
  506.3 14.4 %fusion.218 = (f32[6,128]{1,0:T(8,128)S(1)}, f32[6,128,1024]{2,1,0:T(8,128)S(1)}) fusion(f32[1024]{0:T(1024)S(1)} %copy-done.52, bf16[4096,1024]{1,0:T(8,128)(2,1)} %all-gather.19.cloned.1.call-done, f32[6,128,4096]{2,1,0:T(8,128)} %fusion.22, f32[4096]{0:T(1024)S(1)} %copy-done.49, f32[1024]{0:T(1024)S(1)} %copy-done.53, f32[1024]{0:T(1024)S(1)} %copy-done.46, ...), kind=kOutput, calls=%fused_computation.228 | convolution fusion | flops 6479412224 | bytes 27300864 | tf_op jit(solution)/shard_map/dot_general | solution.py:13
  527.0 22.6 %fusion.222 = (f32[4096]{0:T(1024)S(1)}, bf16[6,128,4096]{2,1,0:T(8,128)(2,1)}) fusion(f32[6,128,4096]{2,1,0:T(8,128)} %fusion.22, f32[4096]{0:T(1024)S(1)} %copy-done.49, bf16[4096,1024]{1,0:T(8,128)(2,1)} %all-gather.19.cloned.1.call-done, f32[6,128]{1,0:T(8,128)S(1)} %negate_multiply_fusion.1, f32[6,128]{1,0:T(8,128)S(1)} %get-tuple-element.40, ...), kind=kOutput, calls=%fused_computation.232 | convolution fusion | flops 6518730752 | bytes 32030720 | tf_op jit(solution)/shard_map/dot_general | solution.py:17
  549.7 13.8 %fusion.211 = (f32[1024]{0:T(1024)S(1)}, f32[6,128]{1,0:T(8,128)S(1)}, f32[6,128,1024]{2,1,0:T(8,128)}) fusion(f32[1024]{0:T(1024)S(1)} %copy-done.46, f32[6,128,1024]{2,1,0:T(8,128)S(1)} %get-tuple-element.47, f32[6,128]{1,0:T(8,128)S(1)} %broadcast_multiply_fusion.1, bf16[1024,4096]{1,0:T(8,128)(2,1)} %all-gather.17.cloned.1.call-done, ...), kind=kOutput, calls=%fused_computation.221 | convolution fusion | flops 6453458944 | bytes 25720832 | tf_op jit(solution)/shard_map/dot_general | solution.py:17
  577.9 7.3 %bitcast_reduce_fusion = (f32[16,64]{1,0:T(8,128)S(1)}, f32[6,16,64,128]{3,2,1,0:T(8,128)}) fusion(bf16[6,128,16,64]{1,3,2,0:T(8,128)(2,1)} %bitcast.214, f32[6,16,128,128]{2,3,1,0:T(8,128)} %get-tuple-element.45, f32[6,16,128]{2,1,0:T(8,128)S(1)} %copy-done.43), kind=kOutput, calls=%fused_computation.64 | convolution fusion | flops 205257728 | bytes 11063296 | tf_op jit(solution)/shard_map/nhqk,nqhd->nkhd/dot_general | solution.py:183
  590.0 6.9 multiply_reduce_fusion.1
  596.9 7.0 %multiply_convert_fusion.2 = bf16[6,16,128,128]{2,3,1,0:T(8,128)(2,1)S(1)} fusion(f32[6,16,128,128]{2,3,1,0:T(8,128)} %get-tuple-element.58, f32[6,16,128]{2,1,0:T(8,128)S(1)} %get-tuple-element.57, f32[6,16,128,128]{2,3,1,0:T(8,128)} %get-tuple-element.45, f32[6,16,128]{2,1,0:T(8,128)S(1)} %copy-done.43), kind=kLoop, calls=%fused_computation.32 | loop fusion | flops 6291456 | bytes 15826944 | tf_op jit(solution)/shard_map/convert_element_type | solution.py:174
  617.9 10.3 %fusion.80 = f32[6,128,1024]{2,1,0:T(8,128)S(1)} fusion(f32[6,128,1024]{1,2,0:T(8,128)S(1)} %bitcast.222, bf16[1024,1024]{1,0:T(8,128)(2,1)S(1)} %copy-done.27), kind=kOutput, calls=%fused_computation.113 | convolution fusion | flops 9663676416 | bytes 8388608 | tf_op jit(solution)/shard_map/dot_general | solution.py:23
  628.2 10.2 %fusion.64 = f32[6,128,1024]{2,1,0:T(8,128)S(1)} fusion(f32[6,128,1024]{1,2,0:T(8,128)S(1)} %bitcast.204, bf16[1024,1024]{1,0:T(8,128)(2,1)S(1)} %copy-done.24), kind=kOutput, calls=%fused_computation.97 | convolution fusion | flops 9663676416 | bytes 8388608 | tf_op jit(solution)/shard_map/dot_general | solution.py:23
  643.4 40.4 %all-reduce = (f32[1024]{0:T(1024)}, f32[1024]{0:T(1024)}, f32[1024]{0:T(1024)}, f32[4096]{0:T(1024)}, f32[1024]{0:T(1024)}, /*index=5*/f32[1024]{0:T(1024)}, f32[1024]{0:T(1024)}) all-reduce(f32[1024]{0:T(1024)S(1)} %reshape.235, f32[1024]{0:T(1024)S(1)} %add.370, ...), channel_id=1, replica_groups=mesh['dp'=8,'seq'=4] {'dp','seq'}, use_global_device_ids=true, to_apply=%region_25.26 | all-reduce | flops 10240 | bytes 81920 | tf_op jit(solution)/shard_map/psum | solution.py:54
  (223 shorter events, 128.7 us)
Async XLA Ops:
  7.2 121.8 %copy-start.35 = (bf16[2,128,1024]{2,1,0:T(8,128)(2,1)S(1)}, bf16[2,128,1024]{2,1,0:T(8,128)(2,1)}, u32[]{:S(2)}) copy-start(bf16[2,128,1024]{2,1,0:T(8,128)(2,1)} %param.22) | copy-start | bytes 1572868
  7.2 63.2 %all-gather.9.cloned.1.call-start = ((), (), s32[]{:S(2)}) async-start(), calls=%async_computation.2 | async-start | bytes 2162688 | tf_op jit(solution)/shard_map/all_gather | solution.py:252
  8.9 120.1 %all-gather.13.cloned.1.call-start = ((), (), s32[]{:S(2)}) async-start(), calls=%async_computation.4 | async-start | bytes 2162688 | tf_op jit(solution)/shard_map/all_gather | solution.py:251
  10.5 177.1 %all-gather.11.cloned.1.call-start = ((), (), s32[]{:S(2)}) async-start(), calls=%async_computation.3 | async-start | bytes 2162688 | tf_op jit(solution)/shard_map/all_gather | solution.py:250
  12.1 233.3 %all-gather.15.cloned.1.call-start = ((), (), s32[]{:S(2)}) async-start(), calls=%async_computation.5 | async-start | bytes 2162688 | tf_op jit(solution)/shard_map/all_gather | solution.py:253
  13.7 255.1 %all-gather.21.cloned.1.call-start = ((), (), s32[]{:S(2)}) async-start(), calls=%async_computation.8 | async-start | bytes 2621440 | tf_op jit(solution)/shard_map/all_gather | solution.py:49
  73.6 58.6 %copy-start.37 = (f32[32,4096]{1,0:T(8,128)S(1)}, f32[32,4096]{1,0:T(8,128)}, u32[]{:S(2)}) copy-start(f32[32,4096]{1,0:T(8,128)} %param.31) | copy-start | bytes 1572868
  73.6 59.4 %copy-start.38 = (f32[128,1024]{1,0:T(8,128)S(1)}, f32[128,1024]{1,0:T(8,128)}, u32[]{:S(2)}) copy-start(f32[128,1024]{1,0:T(8,128)} %param.32) | copy-start | bytes 1572868
  73.6 60.2 %copy-start.54 = (s32[6]{0:T(128)S(1)}, s32[6]{0:T(128)}, u32[]{:S(2)}) copy-start(s32[6]{0:T(128)} %param.25) | copy-start | bytes 76
  73.7 60.3 %copy-start.48 = (s32[2]{0:T(128)S(1)}, s32[2]{0:T(128)}, u32[]{:S(2)}) copy-start(s32[2]{0:T(128)} %param.26) | copy-start | bytes 28
  73.7 113.9 %copy-start.51 = (f32[1024]{0:T(1024)S(1)}, f32[1024]{0:T(1024)}, u32[]{:S(2)}) copy-start(f32[1024]{0:T(1024)} %param.33) | copy-start | bytes 12292
  73.7 219.2 %all-gather.23.cloned.1.call-start = ((), (), s32[]{:S(2)}) async-start(), calls=%async_computation.9 | async-start | bytes 2621440 | tf_op jit(solution)/shard_map/all_gather | solution.py:48
  132.1 240.7 %all-gather.17.cloned.1.call-start = ((), (), s32[]{:S(2)}) async-start(), calls=%async_computation.6 | async-start | bytes 8650752 | tf_op jit(solution)/shard_map/all_gather | solution.py:254
  132.9 57.9 %copy-start.23 = (bf16[6,128,1024]{2,1,0:T(8,128)(2,1)S(1)}, bf16[6,128,1024]{2,1,0:T(8,128)(2,1)}, u32[]{:S(2)}) copy-start(bf16[6,128,1024]{2,1,0:T(8,128)(2,1)} %param.21) | copy-start | bytes 4718596
  132.9 57.9 %copy-start.50 = (f32[1024]{0:T(1024)S(1)}, f32[1024]{0:T(1024)}, u32[]{:S(2)}) copy-start(f32[1024]{0:T(1024)} %param.34) | copy-start | bytes 12292
  133.0 318.4 %all-gather.19.cloned.1.call-start = ((), (), s32[]{:S(2)}) async-start(), calls=%async_computation.7 | async-start | bytes 8650752 | tf_op jit(solution)/shard_map/all_gather | solution.py:255
  133.8 508.4 %reduce-scatter.5.cloned.1.call-start = ((), (), s32[]{:S(2)}) async-start(), calls=%async_computation.11 | async-start | bytes 2621440 | tf_op jit(solution)/shard_map/reduce_scatter | solution.py:68
  310.8 62.0 %copy-start.46 = (f32[1024]{0:T(1024)S(1)}, f32[1024]{0:T(1024)}, u32[]{:S(2)}) copy-start(f32[1024]{0:T(1024)} %param.38) | copy-start | bytes 12292
  310.8 62.0 %copy-start.49 = (f32[4096]{0:T(1024)S(1)}, f32[4096]{0:T(1024)}, u32[]{:S(2)}) copy-start(f32[4096]{0:T(1024)} %param.36) | copy-start | bytes 49156
  310.8 62.0 %copy-start.53 = (f32[1024]{0:T(1024)S(1)}, f32[1024]{0:T(1024)}, u32[]{:S(2)}) copy-start(f32[1024]{0:T(1024)} %param.39) | copy-start | bytes 12292
  312.9 138.5 %copy-start.52 = (f32[1024]{0:T(1024)S(1)}, f32[1024]{0:T(1024)}, u32[]{:S(2)}) copy-start(f32[1024]{0:T(1024)} %param.37) | copy-start | bytes 12292
  380.9 78.3 %copy-start.40 = (f32[1024]{0:T(1024)S(1)}, f32[1024]{0:T(1024)}, u32[]{:S(2)}) copy-start(f32[1024]{0:T(1024)} %param.40) | copy-start | bytes 12292
  493.2 190.5 %reduce-scatter.3.cloned.1.call-start = ((), (), s32[]{:S(2)}) async-start(), calls=%async_computation.10 | async-start | bytes 2621440 | tf_op jit(solution)/shard_map/reduce_scatter | solution.py:65
  527.0 36.4 %copy-start = (bf16[2,16,128,512]{3,2,1,0:T(8,128)(2,1)}, bf16[2,16,128,512]{3,2,1,0:T(8,128)(2,1)S(1)}, u32[]{:S(2)}) copy-start(bf16[2,16,128,512]{3,2,1,0:T(8,128)(2,1)S(1)} %multiply_convert_fusion.1) | copy-start | bytes 12582916
  (47 other events, 296.8 us)
Sparse Core Ops, SparseCore 0:
  11.4 58.9 all-gather.8
  73.9 55.0 all-gather.12
  132.4 55.0 all-gather.10
  190.3 55.0 all-gather.14
  247.4 21.4 all-gather.20
  270.2 22.5 all-gather.22
  295.7 77.0 all-gather.16
  375.7 75.6 all-gather.18
  493.3 29.7 reduce-scatter.4
  597.0 29.7 reduce-scatter.2
where the time goes:
time: 704 us; the launch traced here: 695 us
  waiting for transfers between devices  360 us (51%)
  matrix products  211 us (30%)
  blocking collectives  40.4 us (6%)
  local copies, waits for them, and re-layouts  34.1 us (5%)
  other arithmetic  33 us (5%)
  between operations  15.4 us (2%)
    all_gather x1, waiting for transfers between devices, on_device(): lax.all_gather(downward_low, ('dp', 'seq'), axis=0, tiled=True)  70.5 us
    dot_general x12, matrix products, forward_product(): return jnp.dot(left, right, preferred_element_type=jnp.float32)  70.3 us
    all_gather x1, waiting for transfers between devices, on_device(): lax.all_gather(upward_low, ('dp', 'seq'), axis=0, tiled=True)  59.9 us
    all_gather x1, waiting for transfers between devices, on_device(): lax.all_gather(value_low, ('dp', 'seq'), axis=0, tiled=True)  56.7 us
    dot_general x8, matrix products, backward_product(): lax.dot_general(left, right, (((left.ndim - 1,), (1,)), ((), ())), prefer...  55.5 us
    all_gather x1, waiting for transfers between devices, on_device(): lax.all_gather(key_low, ('dp', 'seq'), axis=0, tiled=True)  55.3 us
    all_gather x1, waiting for transfers between devices, on_device(): lax.all_gather(query_low, ('dp', 'seq'), axis=0, tiled=True)  53.6 us
    psum x1, blocking collectives, settle_each(): return lax.psum(value, ('dp', 'seq'))  40.4 us
  transfers between devices with their start and end apart: 10, of which 8 were waited for; matrix products, arithmetic and copies ran while one was open for 32% of the time, Pallas kernels for 0%

commit v1 on v0

--- a/solution.py
+++ b/solution.py
@@ -1,3 +1,4 @@
+import functools
 import jax
 import jax.numpy as jnp
 from jax import lax
@@ -7,6 +8,14 @@
 HEAD = 64
 epsilon = 1e-12
 masked = -1e30
+
+
+def edit_the_halves(local_block, mesh_ax):
+    far_arr = jax.lax.all_gather(local_block, mesh_ax)
+    return jnp.sum(far_arr, axis=0)
+
+
+convert_the_desk = functools.partial(edit_the_halves, mesh_ax=("dp", "seq"))
 
 
 def forward_product(left, right):
@@ -51,7 +60,7 @@
 
 
 def settle_each(value):
-    return lax.psum(value, ("dp", "seq"))
+    return convert_the_desk(value)
 
 
 def finish_local(key_terms, value_terms, key_exact, value_exact, settle):

time: 704 us -> 1200 us (1.70)
  blocking collectives: 40.4 us -> 535 us
    all_gather x0 -> x14, blocking collectives: none -> 535 us  [edit_the_halves(): far_arr = jax.lax.all_gather(local_block, mesh_ax)]
    psum x1 -> x0, blocking collectives: 40.4 us -> none  [settle_each(): return lax.psum(value, ('dp', 'seq'))]
  transfers between devices with their start and end apart: 10 -> 10, of which waited for: 8 -> 8; matrix products, arithmetic and copies ran while one was open for 32% -> 19% of each run, Pallas kernels for 0% -> 0%
where the time goes in v1:
time: 1200 us; the launch traced here: 1190 us
  blocking collectives  535 us (45%)
  waiting for transfers between devices  361 us (30%)
  matrix products  210 us (18%)
  other arithmetic  40.3 us (3%)
  local copies, waits for them, and re-layouts  32.9 us (3%)
  between operations  15.5 us (1%)
    all_gather x14, blocking collectives, edit_the_halves(): far_arr = jax.lax.all_gather(local_block, mesh_ax)  535 us
    all_gather x1, waiting for transfers between devices, on_device(): lax.all_gather(downward_low, ('dp', 'seq'), axis=0, tiled=True)  70.4 us
    dot_general x12, matrix products, forward_product(): return jnp.dot(left, right, preferred_element_type=jnp.float32)  68.6 us
    dot_general x8, matrix products, backward_product(): lax.dot_general(left, right, (((left.ndim - 1,), (1,)), ((), ())), prefer...  60.7 us
    all_gather x1, waiting for transfers between devices, on_device(): lax.all_gather(upward_low, ('dp', 'seq'), axis=0, tiled=True)  60 us
    all_gather x1, waiting for transfers between devices, on_device(): lax.all_gather(value_low, ('dp', 'seq'), axis=0, tiled=True)  56.7 us
    all_gather x1, waiting for transfers between devices, on_device(): lax.all_gather(key_low, ('dp', 'seq'), axis=0, tiled=True)  55.3 us
    all_gather x1, waiting for transfers between devices, on_device(): lax.all_gather(query_low, ('dp', 'seq'), axis=0, tiled=True)  53.5 us
  transfers between devices with their start and end apart: 10, of which 8 were waited for; matrix products, arithmetic and copies ran while one was open for 19% of the time, Pallas kernels for 0%

profile of v1, /device:TPU:0, one launch (start us, length us, event | category | flops | bytes accessed | tf_op | source)
XLA Modules:
  0.0 1194.9 jit_solution(9154295597155534078)
XLA Ops:
  13.8 56.7 %all-gather.23.cloned.1.call-done = bf16[1024,1024]{1,0:T(8,128)(2,1)} async-done(((bf16[32,1024]{1,0:T(8,128)(2,1)}), bf16[1024,1024]{1,0:T(8,128)(2,1)}) %all-gather.23.cloned.1.call-update) | async-done | bytes 2097168 | tf_op jit(solution)/shard_map/all_gather | solution.py:261
  73.7 55.3 %all-gather.27.cloned.1.call-done = bf16[1024,1024]{1,0:T(8,128)(2,1)} async-done(((bf16[32,1024]{1,0:T(8,128)(2,1)}), bf16[1024,1024]{1,0:T(8,128)(2,1)}) %all-gather.27.cloned.1.call-update) | async-done | bytes 2097168 | tf_op jit(solution)/shard_map/all_gather | solution.py:260
  134.0 53.5 %all-gather.25.cloned.1.call-done = bf16[1024,1024]{1,0:T(8,128)(2,1)} async-done(((bf16[32,1024]{1,0:T(8,128)(2,1)}), bf16[1024,1024]{1,0:T(8,128)(2,1)}) %all-gather.25.cloned.1.call-update) | async-done | bytes 2097168 | tf_op jit(solution)/shard_map/all_gather | solution.py:259
  219.2 26.2 %all-gather.29.cloned.1.call-done = bf16[1024,1024]{1,0:T(8,128)(2,1)} async-done(((bf16[32,1024]{1,0:T(8,128)(2,1)}), bf16[1024,1024]{1,0:T(8,128)(2,1)}) %all-gather.29.cloned.1.call-update) | async-done | bytes 2097168 | tf_op jit(solution)/shard_map/all_gather | solution.py:262
  250.4 18.4 %all-gather.35.cloned.1.call-done = bf16[2,512,1024]{2,1,0:T(8,128)(2,1)} async-done(((bf16[2,128,1024]{2,1,0:T(8,128)(2,1)}), bf16[2,512,1024]{2,1,0:T(8,128)(2,1)}) %all-gather.35.cloned.1.call-update) | async-done | bytes 2097168 | tf_op jit(solution)/shard_map/all_gather | solution.py:58
  272.8 20.1 %all-gather.37.cloned.1.call-done = bf16[2,512,1024]{2,1,0:T(8,128)(2,1)} async-done(((bf16[2,128,1024]{2,1,0:T(8,128)(2,1)}), bf16[2,512,1024]{2,1,0:T(8,128)(2,1)}) %all-gather.37.cloned.1.call-update) | async-done | bytes 2097168 | tf_op jit(solution)/shard_map/all_gather | solution.py:57
  312.8 60.0 %all-gather.31.cloned.1.call-done = bf16[1024,4096]{1,0:T(8,128)(2,1)} async-done(((bf16[32,4096]{1,0:T(8,128)(2,1)}), bf16[1024,4096]{1,0:T(8,128)(2,1)}) %all-gather.31.cloned.1.call-update) | async-done | bytes 8388624 | tf_op jit(solution)/shard_map/all_gather | solution.py:263
  380.9 70.4 %all-gather.33.cloned.1.call-done = bf16[4096,1024]{1,0:T(8,128)(2,1)} async-done(((bf16[128,1024]{1,0:T(8,128)(2,1)}), bf16[4096,1024]{1,0:T(8,128)(2,1)}) %all-gather.33.cloned.1.call-update) | async-done | bytes 8388624 | tf_op jit(solution)/shard_map/all_gather | solution.py:264
  494.7 43.3 %all-gather.4 = f32[131072]{0:T(1024)} all-gather(f32[4096]{0:T(1024)S(1)} %get-tuple-element.60), channel_id=6, replica_groups=mesh['dp'=8,'seq'=4] {'dp','seq'}, dimensions={0}, use_global_device_ids=true | all-gather | bytes 540672 | tf_op jit(solution)/shard_map/all_gather | solution.py:14
  539.9 37.0 %all-gather.2 = f32[32768]{0:T(1024)S(1)} all-gather(f32[1024]{0:T(1024)S(1)} %add_reduce_fusion.2), channel_id=4, replica_groups=mesh['dp'=8,'seq'=4] {'dp','seq'}, dimensions={0}, use_global_device_ids=true | all-gather | bytes 135168 | tf_op jit(solution)/shard_map/all_gather | solution.py:14
  590.4 16.3 %fusion.218 = (f32[6,128]{1,0:T(8,128)S(1)}, f32[6,128,1024]{2,1,0:T(8,128)S(1)}) fusion(f32[1024]{0:T(1024)S(1)} %copy-done.58, bf16[4096,1024]{1,0:T(8,128)(2,1)} %all-gather.33.cloned.1.call-done, f32[6,128,4096]{2,1,0:T(8,128)S(1)} %fusion.22, f32[4096]{0:T(1024)S(1)} %copy-done.55, f32[1024]{0:T(1024)S(1)} %copy-done.59, f32[1024]{0:T(1024)S(1)} %copy-done.43, ...), kind=kOutput, calls=%fused_computation.228 | convolution fusion | flops 6479412224 | bytes 27300864 | tf_op jit(solution)/shard_map/dot_general | solution.py:22
  608.8 21.7 %fusion.222 = (f32[4096]{0:T(1024)}, bf16[6,128,4096]{2,1,0:T(8,128)(2,1)}) fusion(f32[6,128,4096]{2,1,0:T(8,128)} %copy-done.63, f32[4096]{0:T(1024)S(1)} %copy-done.55, bf16[4096,1024]{1,0:T(8,128)(2,1)} %all-gather.33.cloned.1.call-done, f32[6,128]{1,0:T(8,128)S(1)} %negate_multiply_fusion.1, f32[6,128]{1,0:T(8,128)S(1)} %get-tuple-element.33, ...), kind=kOutput, calls=%fused_computation.232 | convolution fusion | flops 6518730752 | bytes 32030720 | tf_op jit(solution)/shard_map/dot_general | solution.py:26
  649.4 38.3 %all-gather.10 = f32[32768]{0:T(1024)S(1)} all-gather(f32[1024]{0:T(1024)S(1)} %get-tuple-element.21), channel_id=12, replica_groups=mesh['dp'=8,'seq'=4] {'dp','seq'}, dimensions={0}, use_global_device_ids=true | all-gather | bytes 135168 | tf_op jit(solution)/shard_map/all_gather | solution.py:14
  690.3 37.4 %all-gather.8 = f32[32768]{0:T(1024)S(1)} all-gather(f32[1024]{0:T(1024)} %get-tuple-element.19), channel_id=10, replica_groups=mesh['dp'=8,'seq'=4] {'dp','seq'}, dimensions={0}, use_global_device_ids=true | all-gather | bytes 135168 | tf_op jit(solution)/shard_map/all_gather | solution.py:14
  727.7 38.5 %all-gather.6 = f32[32768]{0:T(1024)S(1)} all-gather(f32[1024]{0:T(1024)} %get-tuple-element.22), channel_id=8, replica_groups=mesh['dp'=8,'seq'=4] {'dp','seq'}, dimensions={0}, use_global_device_ids=true | all-gather | bytes 135168 | tf_op jit(solution)/shard_map/all_gather | solution.py:14
  771.1 37.4 %all-gather.12 = f32[32,1,1024]{2,1,0:T(1,128)S(1)} all-gather(f32[1,1,1024]{2,1,0:T(1,128)S(1)} %reshape.251), channel_id=1, replica_groups=mesh['dp'=8,'seq'=4] {'dp','seq'}, dimensions={0}, use_global_device_ids=true | all-gather | bytes 135168 | tf_op jit(solution)/shard_map/all_gather | solution.py:14
  818.1 38.2 %all-gather.1 = f32[32768]{0:T(1024)S(1)} all-gather(f32[1024]{0:T(1024)S(1)} %add_reduce_fusion), channel_id=3, replica_groups=mesh['dp'=8,'seq'=4] {'dp','seq'}, dimensions={0}, use_global_device_ids=true | all-gather | bytes 135168 | tf_op jit(solution)/shard_map/all_gather | solution.py:14
  856.4 37.1 %all-gather.7 = f32[32768]{0:T(1024)S(1)} all-gather(f32[1024]{0:T(1024)S(1)} %copy-done.53), channel_id=9, replica_groups=mesh['dp'=8,'seq'=4] {'dp','seq'}, dimensions={0}, use_global_device_ids=true | all-gather | bytes 135168 | tf_op jit(solution)/shard_map/all_gather | solution.py:14
  897.2 38.3 %all-gather.9 = f32[32768]{0:T(1024)S(1)} all-gather(f32[1024]{0:T(1024)S(1)} %get-tuple-element.15), channel_id=11, replica_groups=mesh['dp'=8,'seq'=4] {'dp','seq'}, dimensions={0}, use_global_device_ids=true | all-gather | bytes 135168 | tf_op jit(solution)/shard_map/all_gather | solution.py:14
  935.6 37.1 %all-gather.5 = f32[32768]{0:T(1024)S(1)} all-gather(f32[1024]{0:T(1024)S(1)} %get-tuple-element.16), channel_id=7, replica_groups=mesh['dp'=8,'seq'=4] {'dp','seq'}, dimensions={0}, use_global_device_ids=true | all-gather | bytes 135168 | tf_op jit(solution)/shard_map/all_gather | solution.py:14
  972.8 39.3 %all-gather.3 = f32[131072]{0:T(1024)S(1)} all-gather(f32[4096]{0:T(1024)S(1)} %copy-done.49), channel_id=5, replica_groups=mesh['dp'=8,'seq'=4] {'dp','seq'}, dimensions={0}, use_global_device_ids=true | all-gather | bytes 540672 | tf_op jit(solution)/shard_map/all_gather | solution.py:14
  1019.1 37.0 %all-gather.13 = f32[32,1,1024]{2,1,0:T(1,128)S(1)} all-gather(f32[1,1,1024]{2,1,0:T(1,128)S(1)} %reshape.253), channel_id=1, replica_groups=mesh['dp'=8,'seq'=4] {'dp','seq'}, dimensions={0}, use_global_device_ids=true | all-gather | bytes 135168 | tf_op jit(solution)/shard_map/all_gather | solution.py:14
  1072.6 38.5 %all-gather.11 = f32[32,1,1024]{2,1,0:T(1,128)S(1)} all-gather(f32[1,1,1024]{2,1,0:T(1,128)S(1)} %reshape.249), channel_id=1, replica_groups=mesh['dp'=8,'seq'=4] {'dp','seq'}, dimensions={0}, use_global_device_ids=true | all-gather | bytes 135168 | tf_op jit(solution)/shard_map/all_gather | solution.py:14
  1146.1 37.3 %all-gather = f32[32768]{0:T(1024)S(1)} all-gather(f32[1024]{0:T(1024)S(1)} %convert_reduce_fusion.2), channel_id=2, replica_groups=mesh['dp'=8,'seq'=4] {'dp','seq'}, dimensions={0}, use_global_device_ids=true | all-gather | bytes 135168 | tf_op jit(solution)/shard_map/all_gather | solution.py:14
  (276 shorter events, 245.8 us)
Async XLA Ops:
  7.2 121.8 %copy-start.31 = (bf16[2,128,1024]{2,1,0:T(8,128)(2,1)S(1)}, bf16[2,128,1024]{2,1,0:T(8,128)(2,1)}, u32[]{:S(2)}) copy-start(bf16[2,128,1024]{2,1,0:T(8,128)(2,1)} %param.22) | copy-start | bytes 1572868
  7.2 63.2 %all-gather.23.cloned.1.call-start = ((), (), s32[]{:S(2)}) async-start(), calls=%async_computation.2 | async-start | bytes 2162688 | tf_op jit(solution)/shard_map/all_gather | solution.py:261
  8.8 120.1 %all-gather.27.cloned.1.call-start = ((), (), s32[]{:S(2)}) async-start(), calls=%async_computation.4 | async-start | bytes 2162688 | tf_op jit(solution)/shard_map/all_gather | solution.py:260
  10.5 177.1 %all-gather.25.cloned.1.call-start = ((), (), s32[]{:S(2)}) async-start(), calls=%async_computation.3 | async-start | bytes 2162688 | tf_op jit(solution)/shard_map/all_gather | solution.py:259
  12.1 233.3 %all-gather.29.cloned.1.call-start = ((), (), s32[]{:S(2)}) async-start(), calls=%async_computation.5 | async-start | bytes 2162688 | tf_op jit(solution)/shard_map/all_gather | solution.py:262
  13.7 255.1 %all-gather.35.cloned.1.call-start = ((), (), s32[]{:S(2)}) async-start(), calls=%async_computation.8 | async-start | bytes 2621440 | tf_op jit(solution)/shard_map/all_gather | solution.py:58
  73.7 113.9 %copy-start.57 = (f32[1024]{0:T(1024)S(1)}, f32[1024]{0:T(1024)}, u32[]{:S(2)}) copy-start(f32[1024]{0:T(1024)} %param.33) | copy-start | bytes 12292
  73.7 219.2 %all-gather.37.cloned.1.call-start = ((), (), s32[]{:S(2)}) async-start(), calls=%async_computation.9 | async-start | bytes 2621440 | tf_op jit(solution)/shard_map/all_gather | solution.py:57
  132.1 240.7 %all-gather.31.cloned.1.call-start = ((), (), s32[]{:S(2)}) async-start(), calls=%async_computation.6 | async-start | bytes 8650752 | tf_op jit(solution)/shard_map/all_gather | solution.py:263
  133.0 318.4 %all-gather.33.cloned.1.call-start = ((), (), s32[]{:S(2)}) async-start(), calls=%async_computation.7 | async-start | bytes 8650752 | tf_op jit(solution)/shard_map/all_gather | solution.py:264
  133.8 1011.1 %reduce-scatter.5.cloned.1.call-start = ((), (), s32[]{:S(2)}) async-start(), calls=%async_computation.11 | async-start | bytes 2621440 | tf_op jit(solution)/shard_map/reduce_scatter | solution.py:77
  310.6 62.2 %copy-start.43 = (f32[1024]{0:T(1024)S(1)}, f32[1024]{0:T(1024)}, u32[]{:S(2)}) copy-start(f32[1024]{0:T(1024)} %param.38) | copy-start | bytes 12292
  310.6 62.2 %copy-start.55 = (f32[4096]{0:T(1024)S(1)}, f32[4096]{0:T(1024)}, u32[]{:S(2)}) copy-start(f32[4096]{0:T(1024)} %param.36) | copy-start | bytes 49156
  312.8 138.6 %copy-start.58 = (f32[1024]{0:T(1024)S(1)}, f32[1024]{0:T(1024)}, u32[]{:S(2)}) copy-start(f32[1024]{0:T(1024)} %param.37) | copy-start | bytes 12292
  380.9 78.3 %copy-start.36 = (f32[1024]{0:T(1024)S(1)}, f32[1024]{0:T(1024)}, u32[]{:S(2)}) copy-start(f32[1024]{0:T(1024)} %param.40) | copy-start | bytes 12292
  581.0 603.0 %reduce-scatter.3.cloned.1.call-start = ((), (), s32[]{:S(2)}) async-start(), calls=%async_computation.10 | async-start | bytes 2621440 | tf_op jit(solution)/shard_map/reduce_scatter | solution.py:74
  689.6 119.0 %copy-start.3 = (f32[6,128,1024]{2,1,0:T(8,128)S(1)}, f32[6,128,1024]{2,1,0:T(8,128)}, u32[]{:S(2)}) copy-start(f32[6,128,1024]{2,1,0:T(8,128)} %get-tuple-element.26) | copy-start | bytes 9437188
  690.2 118.4 %copy-start.48 = (f32[6,128]{1,0:T(8,128)S(1)}, f32[6,128]{1,0:T(8,128)}, u32[]{:S(2)}) copy-start(f32[6,128]{1,0:T(8,128)} %get-tuple-element.25) | copy-start | bytes 9220
  813.2 80.4 %copy-start.1 = (f32[6,128,1024]{2,1,0:T(8,128)S(1)}, f32[6,128,1024]{2,1,0:T(8,128)}, u32[]{:S(2)}) copy-start(f32[6,128,1024]{2,1,0:T(8,128)} %copy-done) | copy-start | bytes 9437188
  813.2 80.4 %copy-start.45 = (f32[1024]{0:T(1024)S(1)}, f32[1024]{0:T(1024)}, u32[]{:S(2)}) copy-start(f32[1024]{0:T(1024)} %param.41) | copy-start | bytes 12292
  813.2 80.4 %copy-start.47 = (f32[6,128]{1,0:T(8,128)S(1)}, f32[6,128]{1,0:T(8,128)}, u32[]{:S(2)}) copy-start(f32[6,128]{1,0:T(8,128)} %copy-done.46) | copy-start | bytes 9220
  893.6 79.1 %copy-start.49 = (f32[4096]{0:T(1024)S(1)}, f32[4096]{0:T(1024)}, u32[]{:S(2)}) copy-start(f32[4096]{0:T(1024)} %get-tuple-element.58) | copy-start | bytes 49156
  897.2 115.0 %copy-start.29 = (bf16[6,128,1024]{1,2,0:T(8,128)(2,1)S(1)}, bf16[6,128,1024]{1,2,0:T(8,128)(2,1)}, u32[]{:S(2)}) copy-start(bf16[6,128,1024]{1,2,0:T(8,128)(2,1)} %copy.109) | copy-start | bytes 4718596
  897.2 115.0 %copy-start.40 = (f32[6,16,128]{2,1,0:T(8,128)S(1)}, f32[6,16,128]{2,1,0:T(8,128)}, u32[]{:S(2)}) copy-start(f32[6,16,128]{2,1,0:T(8,128)} %copy-done.39) | copy-start | bytes 147460
  (54 other events, 1170.1 us)
Sparse Core Ops, SparseCore 0:
  11.4 58.9 all-gather.22
  73.9 55.0 all-gather.26
  132.4 55.0 all-gather.24
  190.3 55.0 all-gather.28
  247.4 21.4 all-gather.34
  270.2 22.5 all-gather.36
  295.7 77.0 all-gather.30
  375.7 75.6 all-gather.32
  581.1 28.6 reduce-scatter.4
  1063.2 29.0 reduce-scatter.2
